TPU v7x, 32 devices: a whole 2x2x4 slice. The times are simulated.
32 devices in a mesh: strip: 8 (over z, y), chan: 4 (over x, core).
Axes of the slice: x: 2, y: 2, z: 4, core: 2. Of those that a mesh axis runs over, the one named last changes fastest.
Arguments:
- activations: bfloat16 [64, 128, 1280], P('strip', None, 'chan'), may hold values from -17 to 17
- weight: bfloat16 [9, 1280, 1280], P(None, None, 'chan'), may hold values from -0.0546875 to 0.0546875
- gamma: float32 [1280], replicated, may hold values from 0.25 to 1.75
- beta: float32 [1280], replicated, may hold values from -3 to 3
- group_map: int32 [1280], replicated, may hold values from 0 to 31, as said below
- lengths: int32 [8], P('strip'), may hold values from 1 to 8, 48 in all
- stale_edges: bfloat16 [16, 128, 1280], P('strip', None, 'chan'), may hold values from -6 to 6
- stale_mean: float32 [32], replicated, may hold values from -0.5 to 0.5
- stale_square: float32 [32], replicated, may hold values from 1 to 4
- old_mean: float32 [8, 32], P('strip'), may hold values from -0.5 to 0.5
- old_square: float32 [8, 32], P('strip'), may hold values from 0.5 to 6
Outputs:
- upsampled: bfloat16 [128, 256, 1280], P('strip', None, 'chan')
- new_mean: float32 [32], replicated
- new_square: float32 [32], replicated
Inputs may be any that keep to these rules, and one draw needn't show every extreme that they name: `group_map`: every group has exactly 40 channels. The lengths sum to 48, and some strip uses all 8 rows.
All inputs are finite; a program needn't handle non-finite values. No bound on the sum of `lengths` on one device may be relied on, other than what follows from the above.
Results may differ from a plain program's by a relative error of at most 0.0027.
Values may be sent and summed in bfloat16 or wider, within the bound.
A program may use at most 64 MiB of HBM per device.

v0:
```python
import jax
import jax.numpy as jnp
from jax import lax
from jax.sharding import PartitionSpec as P

EPS = 1e-05


def padded_2(block, sides, width):
    for axis, dim in sides:
        count = lax.axis_size(axis)
        forward = [(i, i + 1) for i in range(count - 1)]
        backward = [(target, source) for source, target in forward]
        low = lax.ppermute(
            lax.slice_in_dim(block, block.shape[dim] - width, None, axis=dim), axis, forward
        )
        high = lax.ppermute(lax.slice_in_dim(block, 0, width, axis=dim), axis, backward)
        block = jnp.concatenate([low, block, high], axis=dim)
    return block


def per_device(
    activations,
    weight,
    gamma,
    beta,
    group_map,
    lengths,
    stale_edges,
    stale_mean,
    stale_square,
    old_mean,
    old_square,
):
    rows, width, local_c = activations.shape
    channels = weight.shape[1]
    groups = stale_mean.shape[0]
    per_group = channels // groups
    offset = lax.axis_index("chan") * local_c
    member = (group_map[:, None] == jnp.arange(groups, dtype=jnp.int32)[None, :]).astype(
        jnp.float32
    )
    local_member = lax.dynamic_slice_in_dim(member, offset, local_c, 0)
    length = lengths[0]
    used = (jnp.arange(rows, dtype=jnp.int32) < length).astype(jnp.float32)[:, None, None]
    values = activations.astype(jnp.float32) * used
    chan_sum = jnp.sum(values, axis=(0, 1))
    chan_sq = jnp.sum(values * values, axis=(0, 1))
    part_one = jnp.sum(chan_sum[:, None] * local_member, axis=0)
    part_two = jnp.sum(chan_sq[:, None] * local_member, axis=0)
    strip_one, strip_two = lax.psum((part_one, part_two), "chan")
    total_count = float(lax.axis_size("strip") * (3 * rows // 4) * width * per_group)
    image_one, image_two = lax.psum((strip_one, strip_two), "strip")
    new_mean = image_one / total_count
    new_square = image_two / total_count
    count = length.astype(jnp.float32) * (width * per_group)
    fresh_mean = strip_one / count
    fresh_square = strip_two / count
    mean_g = stale_mean + fresh_mean - old_mean[0]
    square_g = stale_square + fresh_square - old_square[0]
    var_g = jnp.maximum(square_g - mean_g * mean_g, 0.5 * (fresh_square - fresh_mean * fresh_mean))
    rstd_g = lax.rsqrt(var_g + EPS)
    scale_c = jnp.sum(member * rstd_g[None, :], axis=1) * gamma
    shift_c = beta - jnp.sum(member * mean_g[None, :], axis=1) * scale_c
    bordered = padded_2(stale_edges, (("strip", 0),), 1)
    bounds = jnp.stack([bordered[0], bordered[3]], axis=0)
    initial = jnp.zeros((rows * width, local_c), jnp.float32)
    total = initial
    piece = lax.all_gather(activations, "chan", axis=2, tiled=True)
    bound = lax.all_gather(bounds, "chan", axis=2, tiled=True)
    depth = piece.shape[2]
    act = (jax.nn.silu(piece.astype(jnp.float32) * scale_c + shift_c) * used).astype(jnp.bfloat16)
    padded = jnp.concatenate([bound[0:1], act, jnp.zeros((1, width, depth), jnp.bfloat16)], axis=0)
    place = (jnp.arange(rows + 2, dtype=jnp.int32) == length + 1)[:, None, None]
    padded = jnp.where(place, bound[1][None], padded)
    padded = jnp.pad(padded, ((0, 0), (1, 1), (0, 0)))
    for tap in range(9):
        down, across = (tap // 3, tap % 3)
        patch = padded[down : down + rows, across : across + width].reshape(rows * width, depth)
        total = total + jnp.dot(patch, weight[tap], preferred_element_type=jnp.float32)
    block = ((activations.astype(jnp.float32) + total.reshape(rows, width, local_c)) * used).astype(
        jnp.bfloat16
    )
    upsampled = jnp.repeat(jnp.repeat(block, 2, axis=0), 2, axis=1)
    return (upsampled, new_mean, new_square)


def solution(mesh):
    in_specs = (
        P("strip", None, "chan"),
        P(None, None, "chan"),
        P(),
        P(),
        P(),
        P("strip"),
        P("strip", None, "chan"),
        P(),
        P(),
        P("strip", None),
        P("strip", None),
    )
    out_specs = (P("strip", None, "chan"), P(), P())
    return jax.shard_map(
        per_device, mesh=mesh, in_specs=in_specs, out_specs=out_specs, check_vma=False
    )
```

profile of v0, /device:TPU:0, one launch (start us, length us, event | category | flops | bytes accessed | tf_op | source)
XLA Modules:
  0.0 100.3 jit_solution(1135148588902950023)
XLA Ops:
  7.2 0.0 copy-start
  7.2 0.0 copy-start.3
  7.2 0.0 copy-start.6
  7.2 0.0 copy-start.8
  7.2 0.0 copy-start.7
  7.2 0.0 copy-start.9
  7.2 0.0 copy-start.4
  7.2 0.0 copy-start.5
  7.2 0.0 all-gather.2.cloned.1.call-start
  7.3 2.4 %copy.49 = bf16[8,128,320]{1,0,2:T(8,128)(2,1)} copy(bf16[8,128,320]{1,2,0:T(8,128)(2,1)} %param.11) | data formatting | bytes 1310720 | tf_op args[0]
  9.7 0.0 all-gather.2.cloned.1.call-update
  9.7 0.9 fusion.30
  10.7 0.1 copy.55
  10.8 1.3 %collective-permute-start.1 = (bf16[1,128,320]{1,0,2:T(2,128)(2,1)S(1)}, bf16[1,128,320]{1,0,2:T(2,128)(2,1)S(1)}, u32[]{:S(2)}, u32[]{:S(2)}) collective-permute-start(bf16[1,128,320]{1,0,2:T(2,128)(2,1)S(1)} %copy.55), channel_id=1, source_target_pairs={{4,0},{8,4},{12,8},{16,12},{20,16},{24,20},{28,24},{5,1},{9,5},{13... | collective-permute-start | bytes 245768 | tf_op jit(solution)/shard_map/ppermute | solution.py:17
  12.1 0.1 copy.54
  12.2 5.5 %collective-permute-start = (bf16[1,128,320]{1,0,2:T(2,128)(2,1)S(1)}, bf16[1,128,320]{1,0,2:T(2,128)(2,1)S(1)}, u32[]{:S(2)}, u32[]{:S(2)}) collective-permute-start(bf16[1,128,320]{1,0,2:T(2,128)(2,1)S(1)} %copy.54), channel_id=1, source_target_pairs={{0,4},{4,8},{8,12},{12,16},{16,20},{20,24},{24,28},{1,5},{5,9},{9,... | collective-permute-start | bytes 245768 | tf_op jit(solution)/shard_map/ppermute | solution.py:14
  18.4 0.1 pad.7.clone
  18.5 0.0 copy-done
  18.5 0.4 fusion.3
  18.9 0.0 copy-done.3
  18.9 0.2 fusion.26
  19.1 7.3 %all-reduce.2 = (f32[32]{0:T(128)S(1)}, f32[32]{0:T(128)S(1)}) all-reduce(f32[32]{0:T(128)S(1)} %get-tuple-element.21, f32[32]{0:T(128)S(1)} %get-tuple-element.20), channel_id=1, replica_groups=mesh['strip'=8,'chan'=4] {'chan'}, use_global_device_ids=true, to_apply=%region_5.0 | all-reduce | flops 64 | bytes 512 | tf_op jit(solution)/shard_map/psum | solution.py:51
  26.5 19.8 %all-reduce.1 = (f32[32]{0:T(128)S(1)}, f32[32]{0:T(128)S(1)}) all-reduce(f32[32]{0:T(128)S(1)} %get-tuple-element.26, f32[32]{0:T(128)S(1)} %get-tuple-element.27), channel_id=1, replica_groups=mesh['strip'=8,'chan'=4] {'strip'}, use_global_device_ids=true, to_apply=%region_8.0 | all-reduce | flops 64 | bytes 512 | tf_op jit(solution)/shard_map/psum | solution.py:53
  46.2 0.0 copy-done.6
  46.2 0.0 copy-done.8
  46.2 0.0 copy-done.7
  46.2 0.0 copy-done.9
  46.3 0.1 select_reduce_fusion.1
  46.4 0.5 broadcast_multiply_fusion
  46.9 0.0 copy-done.4
  46.9 0.0 copy-done.5
  46.9 0.0 collective-permute-done.1
  47.0 0.0 collective-permute-done
  47.0 0.4 pad_maximum_fusion
  47.3 7.5 %all_gather.6 = bf16[2,128,1280]{1,0,2:T(2,128)(2,1)S(1)} all-gather(bf16[2,128,320]{1,0,2:T(2,128)(2,1)S(1)} %pad_maximum_fusion), channel_id=1, replica_groups=mesh['strip'=8,'chan'=4] {'chan'}, dimensions={2}, use_global_device_ids=true | all-gather | bytes 819200 | tf_op jit(solution)/shard_map/all_gather | solution.py:70
  54.9 0.9 fusion.29
  55.8 1.1 %copy.56 = bf16[1,128,1280]{2,1,0:T(8,128)(2,1)} copy(bf16[1,128,1280]{1,0,2:T(2,128)(2,1)S(1)} %get-tuple-element.41) | data formatting | bytes 655360
  56.9 1.1 %copy.57 = bf16[1,128,1280]{2,1,0:T(8,128)(2,1)} copy(bf16[1,128,1280]{1,0,2:T(2,128)(2,1)S(1)} %get-tuple-element.42) | data formatting | bytes 655360
  58.0 3.8 %copy.50 = bf16[8,128,1280]{2,1,0:T(8,128)(2,1)S(1)} copy(bf16[8,128,1280]{1,0,2:T(8,128)(2,1)} %all-gather.2.cloned.1.call-done) | data formatting | bytes 5242880 | tf_op jit(solution)/shard_map/all_gather | solution.py:69
  61.8 0.0 copy-start.1
  61.9 0.0 copy-start.2
  61.9 1.7 %multiply_convert_fusion = bf16[8,128,1280]{2,1,0:T(8,128)(2,1)S(1)} fusion(bf16[8,128,1280]{2,1,0:T(8,128)(2,1)S(1)} %copy.50, f32[8]{0:T(128)S(1)} %compare_convert_fusion, f32[1280]{0:T(1024)S(1)} %get-tuple-element.28, f32[1280]{0:T(1024)S(1)} %get-tuple-element.29), kind=kLoop, calls=%fused_computation | loop fusion | flops 11796480 | bytes 5253152 | tf_op jit(solution)/shard_map/convert_element_type | solution.py:72
  63.5 0.0 copy-done.1
  63.5 0.0 copy-done.2
  63.5 0.4 maximum_select_fusion
  64.0 10.0 %pad_slice_fusion = (bf16[8,128,1280]{2,1,0:T(8,128)(2,1)S(1)}, bf16[8,128,1280]{2,1,0:T(8,128)(2,1)S(1)}, bf16[8,128,1280]{2,1,0:T(8,128)(2,1)S(1)}, bf16[8,128...) fusion(bf16[10,128,1280]{2,1,0:T(8,128)(2,1)S(1)} %maximum_sele, ...), kind=kLoop, calls=%fused_computation.2 | loop fusion | bytes 34734080 | tf_op jit(solution)/shard_map/slice | solution.py:79
  74.1 0.0 slice-start
  74.1 2.3 %fusion.14 = f32[1024,320]{0,1:T(8,128)S(1)} fusion(bf16[1024,1280]{1,0:T(8,128)(2,1)S(1)} %bitcast.78, bf16[9,1280,320]{1,2,0:T(8,128)(2,1)} %param.12), kind=kOutput, calls=%fused_computation.32 | convolution fusion | flops 838860800 | bytes 4751360 | tf_op jit(solution)/shard_map/dot_general | solution.py:80
  76.4 0.0 slice-start.1
  76.4 2.3 %convolution_add_fusion.7 = f32[1024,320]{0,1:T(8,128)S(1)} fusion(f32[1024,320]{0,1:T(8,128)S(1)} %fusion.14, bf16[1024,1280]{1,0:T(8,128)(2,1)S(1)} %bitcast.77, bf16[9,1280,320]{1,2,0:T(8,128)(2,1)} %param.12), kind=kOutput, calls=%fused_computation.20 | convolution fusion | flops 839188480 | bytes 6062080 | tf_op jit(solution)/shard_map/dot_general | solution.py:80
  78.8 0.0 slice-done
  78.8 0.0 slice-done.1
  78.8 1.1 %convolution_add_fusion.6 = f32[1024,320]{0,1:T(8,128)S(1)} fusion(f32[1024,320]{0,1:T(8,128)S(1)} %convolution_add_fusion.7, bf16[1024,1280]{1,0:T(8,128)(2,1)S(1)} %bitcast.76, bf16[9,1280,320]{1,2,0:T(8,128)(2,1)S(1)} %bitcast.81), kind=kOutput, calls=%fused_computation.19 | convolution fusion | flops 839188480 | bytes 6062080 | tf_op jit(solution)/shard_map/dot_general | solution.py:80
  79.9 1.0 %convolution_add_fusion.5 = f32[1024,320]{0,1:T(8,128)S(1)} fusion(f32[1024,320]{0,1:T(8,128)S(1)} %convolution_add_fusion.6, bf16[1024,1280]{1,0:T(8,128)(2,1)S(1)} %bitcast.75, bf16[9,1280,320]{1,2,0:T(8,128)(2,1)S(1)} %bitcast.81), kind=kOutput, calls=%fused_computation.18 | convolution fusion | flops 839188480 | bytes 6062080 | tf_op jit(solution)/shard_map/dot_general | solution.py:80
  80.9 1.1 %convolution_add_fusion.4 = f32[1024,320]{0,1:T(8,128)S(1)} fusion(f32[1024,320]{0,1:T(8,128)S(1)} %convolution_add_fusion.5, bf16[1024,1280]{1,0:T(8,128)(2,1)S(1)} %bitcast.74, bf16[9,1280,320]{1,2,0:T(8,128)(2,1)S(1)} %bitcast.81), kind=kOutput, calls=%fused_computation.17 | convolution fusion | flops 839188480 | bytes 6062080 | tf_op jit(solution)/shard_map/dot_general | solution.py:80
  82.0 1.1 %convolution_add_fusion.3 = f32[1024,320]{0,1:T(8,128)S(1)} fusion(f32[1024,320]{0,1:T(8,128)S(1)} %convolution_add_fusion.4, bf16[1024,1280]{1,0:T(8,128)(2,1)S(1)} %bitcast.73, bf16[9,1280,320]{1,2,0:T(8,128)(2,1)S(1)} %bitcast.81), kind=kOutput, calls=%fused_computation.16 | convolution fusion | flops 839188480 | bytes 6062080 | tf_op jit(solution)/shard_map/dot_general | solution.py:80
  83.0 1.1 %convolution_add_fusion.2 = f32[1024,320]{0,1:T(8,128)S(1)} fusion(f32[1024,320]{0,1:T(8,128)S(1)} %convolution_add_fusion.3, bf16[1024,1280]{1,0:T(8,128)(2,1)S(1)} %bitcast.72, bf16[9,1280,320]{1,2,0:T(8,128)(2,1)S(1)} %bitcast.81), kind=kOutput, calls=%fused_computation.15 | convolution fusion | flops 839188480 | bytes 6062080 | tf_op jit(solution)/shard_map/dot_general | solution.py:80
  84.1 1.1 %convolution_add_fusion.1 = f32[1024,320]{0,1:T(8,128)S(1)} fusion(f32[1024,320]{0,1:T(8,128)S(1)} %convolution_add_fusion.2, bf16[1024,1280]{1,0:T(8,128)(2,1)S(1)} %bitcast.71, bf16[9,1280,320]{1,2,0:T(8,128)(2,1)S(1)} %bitcast.81), kind=kOutput, calls=%fused_computation.14 | convolution fusion | flops 839188480 | bytes 6062080 | tf_op jit(solution)/shard_map/dot_general | solution.py:80
  85.2 1.1 %fusion.2 = f32[40,8,8,128]{3,2,1,0:T(8,128)S(1)} fusion(f32[1024,320]{0,1:T(8,128)S(1)} %convolution_add_fusion.1, bf16[1024,1280]{1,0:T(8,128)(2,1)S(1)} %bitcast.70, bf16[9,1280,320]{1,2,0:T(8,128)(2,1)S(1)} %bitcast.81), kind=kOutput, calls=%fused_computation.13 | convolution fusion | flops 839188480 | bytes 6062080 | tf_op jit(solution)/shard_map/dot_general | solution.py:80
  86.2 0.2 fusion.5
  86.5 0.2 broadcast_in_dim.41
  86.7 1.9 %copy.52 = bf16[16,128,320]{2,0,1:T(8,128)(2,1)} copy(bf16[16,128,320]{1,2,0:T(8,128)(2,1)S(1)} %bitcast.69) | data formatting | bytes 2621440 | tf_op jit(solution)/shard_map/reshape | solution.py:84
  88.6 1.7 %broadcast_in_dim.42 = bf16[16,128,2,320]{3,0,2,1:T(8,128)(2,1)S(1)} broadcast(bf16[16,128,320]{2,0,1:T(8,128)(2,1)} %copy.52), dimensions={0,1,3} | broadcast | bytes 3932160 | tf_op jit(solution)/shard_map/broadcast_in_dim | solution.py:84
  90.3 3.1 %copy.53 = bf16[16,256,320]{1,2,0:T(8,128)(2,1)} copy(bf16[16,256,320]{2,0,1:T(8,128)(2,1)S(1)} %bitcast.68) | data formatting | bytes 5242880
  (7 shorter events, 0.1 us)
Async XLA Ops:
  7.2 11.4 %copy-start = (bf16[8,128,320]{1,2,0:T(8,128)(2,1)S(1)}, bf16[8,128,320]{1,2,0:T(8,128)(2,1)}, u32[]{:S(2)}) copy-start(bf16[8,128,320]{1,2,0:T(8,128)(2,1)} %param.11) | copy-start | bytes 1966084
  7.2 11.7 %copy-start.3 = (s32[1280]{0:T(1024)S(1)}, s32[1280]{0:T(1024)}, u32[]{:S(2)}) copy-start(s32[1280]{0:T(1024)} %param.15) | copy-start | bytes 15364
  7.2 39.0 %copy-start.6 = (f32[1,32]{1,0:T(1,128)S(1)}, f32[1,32]{1,0:T(1,128)}, u32[]{:S(2)}) copy-start(f32[1,32]{1,0:T(1,128)} %param.21) | copy-start | bytes 388
  7.2 39.0 %copy-start.8 = (f32[1,32]{1,0:T(1,128)S(1)}, f32[1,32]{1,0:T(1,128)}, u32[]{:S(2)}) copy-start(f32[1,32]{1,0:T(1,128)} %param.20) | copy-start | bytes 388
  7.2 39.0 %copy-start.7 = (f32[32]{0:T(128)S(1)}, f32[32]{0:T(128)}, u32[]{:S(2)}) copy-start(f32[32]{0:T(128)} %param.19) | copy-start | bytes 388
  7.2 39.0 %copy-start.9 = (f32[32]{0:T(128)S(1)}, f32[32]{0:T(128)}, u32[]{:S(2)}) copy-start(f32[32]{0:T(128)} %param.18) | copy-start | bytes 388
  7.2 39.7 %copy-start.4 = (f32[1280]{0:T(1024)S(1)}, f32[1280]{0:T(1024)}, u32[]{:S(2)}) copy-start(f32[1280]{0:T(1024)} %param.14) | copy-start | bytes 15364
  7.2 39.7 %copy-start.5 = (f32[1280]{0:T(1024)S(1)}, f32[1280]{0:T(1024)}, u32[]{:S(2)}) copy-start(f32[1280]{0:T(1024)} %param.13) | copy-start | bytes 15364
  7.2 50.8 %all-gather.2.cloned.1.call-start = ((), (), s32[]{:S(2)}) async-start(), calls=%async_computation | async-start | bytes 3276800 | tf_op jit(solution)/shard_map/all_gather | solution.py:69
  10.8 36.1 %collective-permute-start.1 = (bf16[1,128,320]{1,0,2:T(2,128)(2,1)S(1)}, bf16[1,128,320]{1,0,2:T(2,128)(2,1)S(1)}, u32[]{:S(2)}, u32[]{:S(2)}) collective-permute-start(bf16[1,128,320]{1,0,2:T(2,128)(2,1)S(1)} %copy.55), channel_id=1, source_target_pairs={{4,0},{8,4},{12,8},{16,12},{20,16},{24,20},{28,24},{5,1},{9,5},{13... | collective-permute-start | bytes 245768 | tf_op jit(solution)/shard_map/ppermute | solution.py:17
  12.2 34.7 %collective-permute-start = (bf16[1,128,320]{1,0,2:T(2,128)(2,1)S(1)}, bf16[1,128,320]{1,0,2:T(2,128)(2,1)S(1)}, u32[]{:S(2)}, u32[]{:S(2)}) collective-permute-start(bf16[1,128,320]{1,0,2:T(2,128)(2,1)S(1)} %copy.54), channel_id=1, source_target_pairs={{0,4},{4,8},{8,12},{12,16},{16,20},{20,24},{24,28},{1,5},{5,9},{9,... | collective-permute-start | bytes 245768 | tf_op jit(solution)/shard_map/ppermute | solution.py:14
  61.8 1.7 %copy-start.1 = (bf16[1,128,1280]{2,1,0:T(8,128)(2,1)S(1)}, bf16[1,128,1280]{2,1,0:T(8,128)(2,1)}, u32[]{:S(2)}) copy-start(bf16[1,128,1280]{2,1,0:T(8,128)(2,1)} %copy.56) | copy-start | bytes 983044
  61.9 1.7 %copy-start.2 = (bf16[1,128,1280]{2,1,0:T(8,128)(2,1)S(1)}, bf16[1,128,1280]{2,1,0:T(8,128)(2,1)}, u32[]{:S(2)}) copy-start(bf16[1,128,1280]{2,1,0:T(8,128)(2,1)} %copy.57) | copy-start | bytes 983044
  74.1 4.7 %slice-start = ((s8[7372800]{0:T(1024)(128)(4,1)}), s8[4194304]{0:T(1024)(128)(4,1)S(1)}, s32[]{:S(2)}) async-start(s8[7372800]{0:T(1024)(128)(4,1)} %bitcast.80), calls=%async_computation.1 | async-start | bytes 8388608
  76.4 2.4 %slice-start.1 = ((s8[7372800]{0:T(1024)(128)(4,1)}), s8[3178496]{0:T(1024)(128)(4,1)S(1)}, s32[]{:S(2)}) async-start(s8[7372800]{0:T(1024)(128)(4,1)} %bitcast.80), calls=%async_computation.2 | async-start | bytes 6356992
Sparse Core Ops, SparseCore 0:
  10.2 28.4 all-gather.1
where the time goes:
time: 101 us; the launch traced here: 100 us
  blocking collectives  34.6 us (34%)
  local copies, waits for them, and re-layouts  27.7 us (27%)
  between operations  15.1 us (15%)
  matrix products  12 us (12%)
  starting transfers between devices  6.87 us (7%)
  other arithmetic  3.98 us (4%)
    psum x1, blocking collectives, per_device(): image_one, image_two = lax.psum((strip_one, strip_two), 'strip')  19.8 us
    dot_general x9, matrix products, per_device(): jnp.dot(patch, weight[tap], preferred_element_type=jnp.float32)  12 us
    slice x1, local copies, waits for them, and re-layouts, per_device(): padded[down:down + rows, across:across + width].reshape(rows * width, depth)  10 us
    unnamed x30, local copies, waits for them, and re-layouts  8.07 us
    all_gather x1, blocking collectives, per_device(): bound = lax.all_gather(bounds, 'chan', axis=2, tiled=True)  7.51 us
    psum x1, blocking collectives, per_device(): strip_one, strip_two = lax.psum((part_one, part_two), 'chan')  7.31 us
    ppermute x1, starting transfers between devices, padded_2(): lax.ppermute(lax.slice_in_dim(block, block.shape[dim] - width, None, axis...  5.54 us
    all_gather x1, local copies, waits for them, and re-layouts, per_device(): piece = lax.all_gather(activations, 'chan', axis=2, tiled=True)  3.82 us
  transfers between devices with their start and end apart: 3, of which 0 were waited for; matrix products, arithmetic and copies ran while one was open for 6% of the time, Pallas kernels for 0%

commit v1 on v0

--- a/solution.py
+++ b/solution.py
@@ -67,7 +67,12 @@
     initial = jnp.zeros((rows * width, local_c), jnp.float32)
     total = initial
     piece = lax.all_gather(activations, "chan", axis=2, tiled=True)
-    bound = lax.all_gather(bounds, "chan", axis=2, tiled=True)
+    ring = [bounds]
+    for hop in range(3):
+        ring.append(lax.ppermute(ring[-1], "chan", [(dev, (dev + 1) % 4) for dev in range(4)]))
+    bound = jnp.roll(
+        jnp.concatenate(ring[::-1], axis=2), (lax.axis_index("chan") + 1) * ring[0].shape[2], axis=2
+    )
     depth = piece.shape[2]
     act = (jax.nn.silu(piece.astype(jnp.float32) * scale_c + shift_c) * used).astype(jnp.bfloat16)
     padded = jnp.concatenate([bound[0:1], act, jnp.zeros((1, width, depth), jnp.bfloat16)], axis=0)

time: 101 us -> 105 us (1.040)
  waiting for transfers between devices: 0.02 us -> 9.57 us
  blocking collectives: 34.6 us -> 29.6 us
    ppermute x0 -> x3, waiting for transfers between devices: none -> 9.54 us  [per_device(): lax.ppermute(ring[-1], 'chan', [(dev, (dev + 1) % 4) for dev in range(4)])]
    all_gather x1 -> x0, blocking collectives: 7.51 us -> none  [per_device(): bound = lax.all_gather(bounds, 'chan', axis=2, tiled=True)]
    psum x1, blocking collectives: 19.8 us -> 22.6 us  [per_device(): image_one, image_two = lax.psum((strip_one, strip_two), 'strip')]
    concatenate x0 -> x1, local copies, waits for them, and re-layouts: none -> 2.38 us  [per_device(): jnp.roll(jnp.concatenate(ring[::-1], axis=2), (lax.axis_index('chan') + 1...]
    unnamed x30 -> x29, local copies, waits for them, and re-layouts: 8.07 us -> 5.86 us
    broadcast_in_dim x0 -> x1, local copies, waits for them, and re-layouts: none -> 1.12 us  [per_device(): padded = jnp.where(place, bound[1][None], padded)]
  transfers between devices with their start and end apart: 3 -> 6, of which waited for: 0 -> 2; matrix products, arithmetic and copies ran while one was open for 6% -> 6% of each run, Pallas kernels for 0% -> 0%
where the time goes in v1:
time: 105 us; the launch traced here: 104 us
  blocking collectives  29.6 us (28%)
  local copies, waits for them, and re-layouts  28.1 us (27%)
  between operations  15.1 us (14%)
  matrix products  12 us (11%)
  waiting for transfers between devices  9.57 us (9%)
  starting transfers between devices  6.35 us (6%)
  other arithmetic  3.6 us (3%)
    psum x1, blocking collectives, per_device(): image_one, image_two = lax.psum((strip_one, strip_two), 'strip')  22.6 us
    dot_general x9, matrix products, per_device(): jnp.dot(patch, weight[tap], preferred_element_type=jnp.float32)  12 us
    slice x1, local copies, waits for them, and re-layouts, per_device(): padded[down:down + rows, across:across + width].reshape(rows * width, depth)  10 us
    ppermute x3, waiting for transfers between devices, per_device(): lax.ppermute(ring[-1], 'chan', [(dev, (dev + 1) % 4) for dev in range(4)])  9.54 us
    psum x1, blocking collectives, per_device(): strip_one, strip_two = lax.psum((part_one, part_two), 'chan')  6.92 us
    unnamed x29, local copies, waits for them, and re-layouts  5.86 us
    ppermute x1, starting transfers between devices, padded_2(): lax.ppermute(lax.slice_in_dim(block, block.shape[dim] - width, None, axis...  4.9 us
    all_gather x1, local copies, waits for them, and re-layouts, per_device(): piece = lax.all_gather(activations, 'chan', axis=2, tiled=True)  3.82 us
  transfers between devices with their start and end apart: 6, of which 2 were waited for; matrix products, arithmetic and copies ran while one was open for 6% of the time, Pallas kernels for 0%

profile of v1, /device:TPU:0, one launch (start us, length us, event | category | flops | bytes accessed | tf_op | source)
XLA Modules:
  0.0 104.3 jit_solution(7957578673530825882)
XLA Ops:
  7.2 0.0 copy-start
  7.2 0.0 copy-start.3
  7.2 0.0 copy-start.6
  7.2 0.0 copy-start.8
  7.2 0.0 copy-start.7
  7.2 0.0 copy-start.9
  7.2 0.0 copy-start.4
  7.2 0.0 copy-start.5
  7.2 0.0 all-gather.2.cloned.1.call-start
  7.3 2.4 %copy.36 = bf16[8,128,320]{1,0,2:T(8,128)(2,1)} copy(bf16[8,128,320]{1,2,0:T(8,128)(2,1)} %param.11) | data formatting | bytes 1310720 | tf_op args[0]
  9.7 0.0 all-gather.2.cloned.1.call-update
  9.7 0.9 fusion.29
  10.7 0.1 copy.41
  10.8 4.9 %collective-permute-start = (bf16[1,128,320]{2,1,0:T(8,128)(2,1)S(1)}, bf16[1,128,320]{2,1,0:T(8,128)(2,1)S(1)}, u32[]{:S(2)}, u32[]{:S(2)}) collective-permute-start(bf16[1,128,320]{2,1,0:T(8,128)(2,1)S(1)} %copy.41), channel_id=1, source_target_pairs={{0,4},{4,8},{8,12},{12,16},{16,20},{20,24},{24,28},{1,5},{5,9},{9,... | collective-permute-start | bytes 245768 | tf_op jit(solution)/shard_map/ppermute | solution.py:14
  15.7 0.1 copy.42
  15.8 1.3 %collective-permute-start.1 = (bf16[1,128,320]{2,1,0:T(8,128)(2,1)S(1)}, bf16[1,128,320]{2,1,0:T(8,128)(2,1)S(1)}, u32[]{:S(2)}, u32[]{:S(2)}) collective-permute-start(bf16[1,128,320]{2,1,0:T(8,128)(2,1)S(1)} %copy.42), channel_id=1, source_target_pairs={{4,0},{8,4},{12,8},{16,12},{20,16},{24,20},{28,24},{5,1},{9,5},{13... | collective-permute-start | bytes 245768 | tf_op jit(solution)/shard_map/ppermute | solution.py:17
  17.8 0.0 copy-done
  17.8 0.4 fusion.3
  18.2 0.0 copy-done.3
  18.2 0.2 fusion.26
  18.4 6.9 %all-reduce.2 = (f32[32]{0:T(128)S(1)}, f32[32]{0:T(128)S(1)}) all-reduce(f32[32]{0:T(128)S(1)} %get-tuple-element.18, f32[32]{0:T(128)S(1)} %get-tuple-element.17), channel_id=1, replica_groups=mesh['strip'=8,'chan'=4] {'chan'}, use_global_device_ids=true, to_apply=%region_5.0 | all-reduce | flops 64 | bytes 512 | tf_op jit(solution)/shard_map/psum | solution.py:51
  25.4 0.0 collective-permute-done
  25.4 0.0 collective-permute-done.1
  25.4 0.1 collective-permute-start.2
  25.5 0.0 copy-done.6
  25.5 0.0 copy-done.8
  25.5 0.0 copy-done.7
  25.5 0.0 copy-done.9
  25.5 22.6 %all-reduce.1 = (f32[32]{0:T(128)S(1)}, f32[32]{0:T(128)S(1)}) all-reduce(f32[32]{0:T(128)S(1)} %get-tuple-element.23, f32[32]{0:T(128)S(1)} %get-tuple-element.24), channel_id=1, replica_groups=mesh['strip'=8,'chan'=4] {'strip'}, use_global_device_ids=true, to_apply=%region_8.0 | all-reduce | flops 64 | bytes 512 | tf_op jit(solution)/shard_map/psum | solution.py:53
  48.2 0.1 select_reduce_fusion.1
  48.3 0.0 collective-permute-done.2
  48.3 0.1 collective-permute-start.3
  48.4 0.0 copy-done.4
  48.4 0.0 copy-done.5
  48.4 5.0 %collective-permute-done.3 = bf16[2,128,320]{2,1,0:T(8,128)(2,1)S(1)} collective-permute-done((bf16[2,128,320]{2,1,0:T(8,128)(2,1)S(1)}, bf16[2,128,320]{2,1,0:T(8,128)(2,1)S(1)}, u32[]{:S(2)}, u32[]{:S(2)}) %collective-permute-start.3) | collective-permute-done | bytes 163872 | tf_op jit(solution)/shard_map/ppermute | solution.py:72
  53.5 0.0 collective-permute-start.4
  53.5 0.5 broadcast_multiply_fusion
  54.0 0.1 pad.7.clone
  54.1 4.5 %collective-permute-done.4 = bf16[2,128,320]{2,1,0:T(8,128)(2,1)S(1)} collective-permute-done((bf16[2,128,320]{2,1,0:T(8,128)(2,1)S(1)}, bf16[2,128,320]{2,1,0:T(8,128)(2,1)S(1)}, u32[]{:S(2)}, u32[]{:S(2)}) %collective-permute-start.4) | collective-permute-done | bytes 163872 | tf_op jit(solution)/shard_map/ppermute | solution.py:72
  58.6 2.4 %concatenate.9 = bf16[2,128,2560]{2,1,0:T(8,128)(2,1)S(1)} concatenate(bf16[2,128,320]{2,1,0:T(8,128)(2,1)S(1)} %collective-permute-done.4, bf16[2,128,320]{2,1,0:T(8,128)(2,1)S(1)} %collective-permute-done.3, bf16[2,128,320]{2,1,0:T(8,128)(2,1)S(1)} %collective-permute-done.2, bf16[2,128,320]{2,1,0:T(8,128)(2,1)S(1)} %constant_dynamic-update-slice_fusion, ...), dimensions={2} | concatenate | bytes 2621440 | tf_op jit(solution)/shard_map/jit(_roll_dynamic)/concatenate | solution.py:73
  60.9 1.1 %dynamic-slice_bitcast_fusion = (bf16[128,1280]{1,0:T(8,128)(2,1)}, bf16[1,128,1280]{2,1,0:T(8,128)(2,1)}) fusion(bf16[2,128,2560]{2,1,0:T(8,128)(2,1)S(1)} %concatenate.9, s32[]{:T(128)S(6)} %add.101, s32[]{:T(128)S(6)} %select_n.21), kind=kLoop, calls=%fused_computation.43 | loop fusion | bytes 1310728 | tf_op jit(solution)/shard_map/jit(_where)/broadcast_in_dim | solution.py:80
  62.1 3.8 %copy.37 = bf16[8,128,1280]{2,1,0:T(8,128)(2,1)S(1)} copy(bf16[8,128,1280]{1,0,2:T(8,128)(2,1)} %all-gather.2.cloned.1.call-done) | data formatting | bytes 5242880 | tf_op jit(solution)/shard_map/all_gather | solution.py:69
  65.9 0.0 copy-start.1
  65.9 0.0 copy-start.2
  65.9 1.7 %multiply_convert_fusion = bf16[8,128,1280]{2,1,0:T(8,128)(2,1)S(1)} fusion(bf16[8,128,1280]{2,1,0:T(8,128)(2,1)S(1)} %copy.37, f32[8]{0:T(128)S(1)} %compare_convert_fusion, f32[1280]{0:T(1024)S(1)} %get-tuple-element.25, f32[1280]{0:T(1024)S(1)} %get-tuple-element.26), kind=kLoop, calls=%fused_computation | loop fusion | flops 11796480 | bytes 5253152 | tf_op jit(solution)/shard_map/convert_element_type | solution.py:77
  67.6 0.0 copy-done.1
  67.6 0.4 maximum_select_fusion
  68.1 10.0 %pad_slice_fusion = (bf16[8,128,1280]{2,1,0:T(8,128)(2,1)S(1)}, bf16[8,128,1280]{2,1,0:T(8,128)(2,1)S(1)}, bf16[8,128,1280]{2,1,0:T(8,128)(2,1)S(1)}, bf16[8,128...) fusion(bf16[10,128,1280]{2,1,0:T(8,128)(2,1)S(1)} %maximum_sele, ...), kind=kLoop, calls=%fused_computation.2 | loop fusion | bytes 34734080 | tf_op jit(solution)/shard_map/slice | solution.py:84
  78.1 0.0 slice-start
  78.1 2.3 %fusion.14 = f32[1024,320]{0,1:T(8,128)S(1)} fusion(bf16[1024,1280]{1,0:T(8,128)(2,1)S(1)} %bitcast.79, bf16[9,1280,320]{1,2,0:T(8,128)(2,1)} %param.12), kind=kOutput, calls=%fused_computation.32 | convolution fusion | flops 838860800 | bytes 4751360 | tf_op jit(solution)/shard_map/dot_general | solution.py:85
  80.5 0.0 slice-start.1
  80.5 2.3 %convolution_add_fusion.7 = f32[1024,320]{0,1:T(8,128)S(1)} fusion(f32[1024,320]{0,1:T(8,128)S(1)} %fusion.14, bf16[1024,1280]{1,0:T(8,128)(2,1)S(1)} %bitcast.78, bf16[9,1280,320]{1,2,0:T(8,128)(2,1)} %param.12), kind=kOutput, calls=%fused_computation.20 | convolution fusion | flops 839188480 | bytes 6062080 | tf_op jit(solution)/shard_map/dot_general | solution.py:85
  82.9 1.1 %convolution_add_fusion.6 = f32[1024,320]{0,1:T(8,128)S(1)} fusion(f32[1024,320]{0,1:T(8,128)S(1)} %convolution_add_fusion.7, bf16[1024,1280]{1,0:T(8,128)(2,1)S(1)} %bitcast.77, bf16[9,1280,320]{1,2,0:T(8,128)(2,1)S(1)} %bitcast.81), kind=kOutput, calls=%fused_computation.19 | convolution fusion | flops 839188480 | bytes 6062080 | tf_op jit(solution)/shard_map/dot_general | solution.py:85
  83.9 1.0 %convolution_add_fusion.5 = f32[1024,320]{0,1:T(8,128)S(1)} fusion(f32[1024,320]{0,1:T(8,128)S(1)} %convolution_add_fusion.6, bf16[1024,1280]{1,0:T(8,128)(2,1)S(1)} %bitcast.76, bf16[9,1280,320]{1,2,0:T(8,128)(2,1)S(1)} %bitcast.81), kind=kOutput, calls=%fused_computation.18 | convolution fusion | flops 839188480 | bytes 6062080 | tf_op jit(solution)/shard_map/dot_general | solution.py:85
  85.0 1.1 %convolution_add_fusion.4 = f32[1024,320]{0,1:T(8,128)S(1)} fusion(f32[1024,320]{0,1:T(8,128)S(1)} %convolution_add_fusion.5, bf16[1024,1280]{1,0:T(8,128)(2,1)S(1)} %bitcast.75, bf16[9,1280,320]{1,2,0:T(8,128)(2,1)S(1)} %bitcast.81), kind=kOutput, calls=%fused_computation.17 | convolution fusion | flops 839188480 | bytes 6062080 | tf_op jit(solution)/shard_map/dot_general | solution.py:85
  86.0 1.1 %convolution_add_fusion.3 = f32[1024,320]{0,1:T(8,128)S(1)} fusion(f32[1024,320]{0,1:T(8,128)S(1)} %convolution_add_fusion.4, bf16[1024,1280]{1,0:T(8,128)(2,1)S(1)} %bitcast.74, bf16[9,1280,320]{1,2,0:T(8,128)(2,1)S(1)} %bitcast.81), kind=kOutput, calls=%fused_computation.16 | convolution fusion | flops 839188480 | bytes 6062080 | tf_op jit(solution)/shard_map/dot_general | solution.py:85
  87.1 1.1 %convolution_add_fusion.2 = f32[1024,320]{0,1:T(8,128)S(1)} fusion(f32[1024,320]{0,1:T(8,128)S(1)} %convolution_add_fusion.3, bf16[1024,1280]{1,0:T(8,128)(2,1)S(1)} %bitcast.73, bf16[9,1280,320]{1,2,0:T(8,128)(2,1)S(1)} %bitcast.81), kind=kOutput, calls=%fused_computation.15 | convolution fusion | flops 839188480 | bytes 6062080 | tf_op jit(solution)/shard_map/dot_general | solution.py:85
  88.2 1.1 %convolution_add_fusion.1 = f32[1024,320]{0,1:T(8,128)S(1)} fusion(f32[1024,320]{0,1:T(8,128)S(1)} %convolution_add_fusion.2, bf16[1024,1280]{1,0:T(8,128)(2,1)S(1)} %bitcast.72, bf16[9,1280,320]{1,2,0:T(8,128)(2,1)S(1)} %bitcast.81), kind=kOutput, calls=%fused_computation.14 | convolution fusion | flops 839188480 | bytes 6062080 | tf_op jit(solution)/shard_map/dot_general | solution.py:85
  89.2 1.1 %fusion.2 = f32[40,8,8,128]{3,2,1,0:T(8,128)S(1)} fusion(f32[1024,320]{0,1:T(8,128)S(1)} %convolution_add_fusion.1, bf16[1024,1280]{1,0:T(8,128)(2,1)S(1)} %bitcast.71, bf16[9,1280,320]{1,2,0:T(8,128)(2,1)S(1)} %bitcast.81), kind=kOutput, calls=%fused_computation.13 | convolution fusion | flops 839188480 | bytes 6062080 | tf_op jit(solution)/shard_map/dot_general | solution.py:85
  90.3 0.2 fusion.5
  90.5 0.2 broadcast_in_dim.41
  90.8 1.9 %copy.39 = bf16[16,128,320]{2,0,1:T(8,128)(2,1)} copy(bf16[16,128,320]{1,2,0:T(8,128)(2,1)S(1)} %bitcast.70) | data formatting | bytes 2621440 | tf_op jit(solution)/shard_map/reshape | solution.py:89
  92.6 1.7 %broadcast_in_dim.42 = bf16[16,128,2,320]{3,0,2,1:T(8,128)(2,1)S(1)} broadcast(bf16[16,128,320]{2,0,1:T(8,128)(2,1)} %copy.39), dimensions={0,1,3} | broadcast | bytes 3932160 | tf_op jit(solution)/shard_map/broadcast_in_dim | solution.py:89
  94.3 3.1 %copy.40 = bf16[16,256,320]{1,2,0:T(8,128)(2,1)} copy(bf16[16,256,320]{2,0,1:T(8,128)(2,1)S(1)} %bitcast.69) | data formatting | bytes 5242880
  (12 shorter events, 0.1 us)
Async XLA Ops:
  7.2 10.6 %copy-start = (bf16[8,128,320]{1,2,0:T(8,128)(2,1)S(1)}, bf16[8,128,320]{1,2,0:T(8,128)(2,1)}, u32[]{:S(2)}) copy-start(bf16[8,128,320]{1,2,0:T(8,128)(2,1)} %param.11) | copy-start | bytes 1966084
  7.2 11.0 %copy-start.3 = (s32[1280]{0:T(1024)S(1)}, s32[1280]{0:T(1024)}, u32[]{:S(2)}) copy-start(s32[1280]{0:T(1024)} %param.15) | copy-start | bytes 15364
  7.2 18.3 %copy-start.6 = (f32[1,32]{1,0:T(1,128)S(1)}, f32[1,32]{1,0:T(1,128)}, u32[]{:S(2)}) copy-start(f32[1,32]{1,0:T(1,128)} %param.21) | copy-start | bytes 388
  7.2 18.3 %copy-start.8 = (f32[1,32]{1,0:T(1,128)S(1)}, f32[1,32]{1,0:T(1,128)}, u32[]{:S(2)}) copy-start(f32[1,32]{1,0:T(1,128)} %param.20) | copy-start | bytes 388
  7.2 18.3 %copy-start.7 = (f32[32]{0:T(128)S(1)}, f32[32]{0:T(128)}, u32[]{:S(2)}) copy-start(f32[32]{0:T(128)} %param.19) | copy-start | bytes 388
  7.2 18.3 %copy-start.9 = (f32[32]{0:T(128)S(1)}, f32[32]{0:T(128)}, u32[]{:S(2)}) copy-start(f32[32]{0:T(128)} %param.18) | copy-start | bytes 388
  7.2 41.2 %copy-start.4 = (f32[1280]{0:T(1024)S(1)}, f32[1280]{0:T(1024)}, u32[]{:S(2)}) copy-start(f32[1280]{0:T(1024)} %param.14) | copy-start | bytes 15364
  7.2 41.2 %copy-start.5 = (f32[1280]{0:T(1024)S(1)}, f32[1280]{0:T(1024)}, u32[]{:S(2)}) copy-start(f32[1280]{0:T(1024)} %param.13) | copy-start | bytes 15364
  7.2 54.8 %all-gather.2.cloned.1.call-start = ((), (), s32[]{:S(2)}) async-start(), calls=%async_computation | async-start | bytes 3276800 | tf_op jit(solution)/shard_map/all_gather | solution.py:69
  10.8 14.6 %collective-permute-start = (bf16[1,128,320]{2,1,0:T(8,128)(2,1)S(1)}, bf16[1,128,320]{2,1,0:T(8,128)(2,1)S(1)}, u32[]{:S(2)}, u32[]{:S(2)}) collective-permute-start(bf16[1,128,320]{2,1,0:T(8,128)(2,1)S(1)} %copy.41), channel_id=1, source_target_pairs={{0,4},{4,8},{8,12},{12,16},{16,20},{20,24},{24,28},{1,5},{5,9},{9,... | collective-permute-start | bytes 245768 | tf_op jit(solution)/shard_map/ppermute | solution.py:14
  15.8 9.5 %collective-permute-start.1 = (bf16[1,128,320]{2,1,0:T(8,128)(2,1)S(1)}, bf16[1,128,320]{2,1,0:T(8,128)(2,1)S(1)}, u32[]{:S(2)}, u32[]{:S(2)}) collective-permute-start(bf16[1,128,320]{2,1,0:T(8,128)(2,1)S(1)} %copy.42), channel_id=1, source_target_pairs={{4,0},{8,4},{12,8},{16,12},{20,16},{24,20},{28,24},{5,1},{9,5},{13... | collective-permute-start | bytes 245768 | tf_op jit(solution)/shard_map/ppermute | solution.py:17
  25.4 22.9 %collective-permute-start.2 = (bf16[2,128,320]{2,1,0:T(8,128)(2,1)S(1)}, bf16[2,128,320]{2,1,0:T(8,128)(2,1)S(1)}, u32[]{:S(2)}, u32[]{:S(2)}) collective-permute-start(bf16[2,128,320]{2,1,0:T(8,128)(2,1)S(1)} %constant_dynamic-update-slice_fusion), channel_id=1, source_target_pairs={{0,1},{1,2},{2,3},{3,0},{4,5},{5,6},{6,7},{7,4},{8,9},{9,10},{10,1... | collective-permute-start | bytes 491528 | tf_op jit(solution)/shard_map/ppermute | solution.py:72
  48.3 5.1 %collective-permute-start.3 = (bf16[2,128,320]{2,1,0:T(8,128)(2,1)S(1)}, bf16[2,128,320]{2,1,0:T(8,128)(2,1)S(1)}, u32[]{:S(2)}, u32[]{:S(2)}) collective-permute-start(bf16[2,128,320]{2,1,0:T(8,128)(2,1)S(1)} %collective-permute-done.2), channel_id=1, source_target_pairs={{0,1},{1,2},{2,3},{3,0},{4,5},{5,6},{6,7},{7,4},{8,9},{9,10},{10,1... | collective-permute-start | bytes 491528 | tf_op jit(solution)/shard_map/ppermute | solution.py:72
  53.5 5.1 %collective-permute-start.4 = (bf16[2,128,320]{2,1,0:T(8,128)(2,1)S(1)}, bf16[2,128,320]{2,1,0:T(8,128)(2,1)S(1)}, u32[]{:S(2)}, u32[]{:S(2)}) collective-permute-start(bf16[2,128,320]{2,1,0:T(8,128)(2,1)S(1)} %collective-permute-done.3), channel_id=1, source_target_pairs={{0,1},{1,2},{2,3},{3,0},{4,5},{5,6},{6,7},{7,4},{8,9},{9,10},{10,1... | collective-permute-start | bytes 491528 | tf_op jit(solution)/shard_map/ppermute | solution.py:72
  65.9 1.7 %copy-start.1 = (bf16[128,1280]{1,0:T(8,128)(2,1)S(1)}, bf16[128,1280]{1,0:T(8,128)(2,1)}, u32[]{:S(2)}) copy-start(bf16[128,1280]{1,0:T(8,128)(2,1)} %get-tuple-element.38) | copy-start | bytes 983044
  65.9 1.7 %copy-start.2 = (bf16[1,128,1280]{2,1,0:T(8,128)(2,1)S(1)}, bf16[1,128,1280]{2,1,0:T(8,128)(2,1)}, u32[]{:S(2)}) copy-start(bf16[1,128,1280]{2,1,0:T(8,128)(2,1)} %get-tuple-element.39) | copy-start | bytes 983044
  78.1 4.7 %slice-start = ((s8[7372800]{0:T(1024)(128)(4,1)}), s8[4194304]{0:T(1024)(128)(4,1)S(1)}, s32[]{:S(2)}) async-start(s8[7372800]{0:T(1024)(128)(4,1)} %bitcast.80), calls=%async_computation.1 | async-start | bytes 8388608
  80.5 2.4 %slice-start.1 = ((s8[7372800]{0:T(1024)(128)(4,1)}), s8[3178496]{0:T(1024)(128)(4,1)S(1)}, s32[]{:S(2)}) async-start(s8[7372800]{0:T(1024)(128)(4,1)} %bitcast.80), calls=%async_computation.2 | async-start | bytes 6356992
Sparse Core Ops, SparseCore 0:
  10.2 30.4 all-gather.1
